TPU v7x, 256 devices: a 8x8x2 block of a 8x8x16 slice. The times are simulated.
256 devices in a mesh: groups: 2 (over z), ep: 64 (over y, x), tp: 2 (over core).
Axes of the slice: x: 8, y: 8, z: 2, core: 2. Of those that a mesh axis runs over, the one named last changes fastest.
The devices are a block of a 8x8x16 slice.
Arguments:
- hidden: bfloat16 [2048, 3584], P(('groups', 'ep'), 'tp'), parts along dimension 0, may hold values from -6 to 6
- routes: int32 [2048, 8], P(('groups', 'ep')), parts along dimension 0, may hold values from 0 to 63, as said below
- router_weight: bfloat16 [3584, 64], P('tp'), may hold values from -0.1875 to 0.1875
- gate_weight: bfloat16 [64, 3584, 1024], P('ep', None, 'tp'), may hold values from -0.09375 to 0.09375
- up_weight: bfloat16 [64, 3584, 1024], P('ep', None, 'tp'), may hold values from -0.09375 to 0.09375
- down_weight: bfloat16 [64, 1024, 3584], P('ep', 'tp'), may hold values from -0.1875 to 0.1875
- q_latent: bfloat16 [512, 64, 512], P(('groups', 'ep'), 'tp'), parts along dimension 0, may hold values from -48 to 48
- q_rope: bfloat16 [512, 64, 64], P(('groups', 'ep'), 'tp'), parts along dimension 0, may hold values from -48 to 48
- cache_latent: bfloat16 [512, 256, 512], P(('groups', 'ep')), parts along dimension 0, may hold values from -4 to 4
- cache_rope: bfloat16 [512, 64, 256], P(('groups', 'ep')), parts along dimension 0, may hold values from -4 to 4
- lengths: int32 [512], P(('groups', 'ep')), parts along dimension 0, may hold values from 16 to 256, as said below
Outputs:
- moe_out: bfloat16 [2048, 3584], P(('groups', 'ep'), 'tp'), parts along dimension 0
- attn_latent: bfloat16 [512, 64, 512], P(('groups', 'ep'), 'tp'), parts along dimension 0
There are 2 independent parts, one for each index of `groups`. A program takes and returns all parts, laid end to end along the dimension named above; an argument that names none is the same for every part. Nothing has to cross between parts.
Inputs may be any that keep to these rules, and one draw needn't show every extreme that they name: `routes`: each row names 8 different experts; in each aligned block of 16 rows (the rows of one index of ep) no expert is named more than 8 times, and one expert, the same in every block, is named exactly 8 times in each block. `lengths`: one sequence has 256 live positions and one has 16.
All inputs are finite; a program needn't handle non-finite values.
Results may differ from a plain program's by a relative error of at most 0.0085.
Values may be sent and summed in bfloat16 or wider, within the bound.
No kernel may reach another device: no remote copies, remote signals or barrier semaphores. Data moves between devices by JAX's collectives and lax.ppermute only.
A program may use at most 128 MiB of HBM per device.

v0:
```python
import jax
import jax.numpy as jnp
from jax import lax
from jax.sharding import PartitionSpec as P

softmax_scale = 192.0 ** (-0.5)
routed_scale = 2.5


def gathered_total(value, axis):
    tiles = lax.all_gather(value, axis)
    return tiles.sum(axis=0)


def in_blocks(value, dim, devices):
    lengths = value.shape
    tiles = value.reshape(*lengths[:dim], devices, lengths[dim] // devices, *lengths[dim + 1 :])
    return jnp.moveaxis(tiles, dim, 0)


def sum_at_owner(value, axis, dim):
    devices = lax.axis_size(axis)
    tiles = lax.all_to_all(in_blocks(value, dim, devices), axis, 0, 0, tiled=True)
    return jnp.sum(tiles, axis=0)


def local(
    hidden,
    routes,
    router_weight,
    gate_weight,
    up_weight,
    down_weight,
    q_latent,
    q_rope,
    cache_latent,
    cache_rope,
    lengths,
):
    token_count, top_count = routes.shape
    expert_count = lax.axis_size("ep")
    capacity = min(token_count, 4 * token_count * top_count // expert_count)
    partial_logits = jnp.dot(hidden, router_weight, preferred_element_type=jnp.float32)
    logits = gathered_total(partial_logits, "tp")
    affinity = jax.nn.sigmoid(logits)
    expert_iota = jnp.arange(expert_count, dtype=jnp.int32)
    chosen_mask = routes[:, :, None] == expert_iota[None, None, :]
    chosen = jnp.sum(jnp.where(chosen_mask, affinity[:, None, :], 0.0), axis=2)
    gates = routed_scale * chosen / jnp.sum(chosen, axis=1, keepdims=True)
    flat_mask = chosen_mask.reshape(token_count * top_count, expert_count).astype(jnp.int32)
    earlier = jnp.cumsum(flat_mask, axis=0) - flat_mask
    within = jnp.sum(flat_mask * earlier, axis=1).reshape(token_count, top_count)
    slot_index = routes * capacity + within
    slot_iota = jnp.arange(expert_count * capacity, dtype=jnp.int32)
    placing = jnp.sum(
        (slot_index[None, :, :] == slot_iota[:, None, None]).astype(jnp.int32), axis=2
    )
    placing = placing.astype(jnp.bfloat16)
    outgoing = jnp.dot(placing, hidden, preferred_element_type=jnp.float32).astype(jnp.bfloat16)
    outgoing = outgoing.reshape(expert_count, capacity, hidden.shape[1])
    received = lax.all_to_all(outgoing, "ep", split_axis=0, concat_axis=0, tiled=True)
    received = lax.all_gather(received, "tp", axis=2, tiled=True)
    source_count, slot_count, feature_count = received.shape
    flat_rows = received.reshape(source_count * slot_count, feature_count)
    gate_part = jnp.dot(flat_rows, gate_weight[0], preferred_element_type=jnp.float32)
    up_part = jnp.dot(flat_rows, up_weight[0], preferred_element_type=jnp.float32)
    active = (jax.nn.silu(gate_part) * up_part).astype(jnp.bfloat16)
    partial_out = jnp.dot(active, down_weight[0], preferred_element_type=jnp.float32)
    summed = sum_at_owner(partial_out, "tp", 1).astype(jnp.bfloat16)
    summed = summed.reshape(source_count, slot_count, summed.shape[1])
    returned = lax.all_to_all(summed, "ep", split_axis=0, concat_axis=0, tiled=True)
    scores = jnp.einsum("bhl,bjl->bhj", q_latent, cache_latent, preferred_element_type=jnp.float32)
    scores = scores + jnp.einsum(
        "bhr,brj->bhj", q_rope, cache_rope, preferred_element_type=jnp.float32
    )
    scores = scores * softmax_scale
    position = jnp.arange(cache_latent.shape[1], dtype=jnp.int32)
    live = position[None, None, :] < lengths[:, None, None]
    scores = jnp.where(live, scores, -jnp.inf)
    highest = jnp.max(scores, axis=2, keepdims=True)
    expo = jnp.where(live, jnp.exp(scores - highest), 0.0)
    attn_probs = (expo / jnp.sum(expo, axis=2, keepdims=True)).astype(jnp.bfloat16)
    attn_latent = jnp.einsum(
        "bhj,bjl->bhl", attn_probs, cache_latent, preferred_element_type=jnp.float32
    )
    attn_latent = attn_latent.astype(jnp.bfloat16)
    returned_flat = returned.reshape(expert_count * capacity, returned.shape[2])
    picked = jnp.take(returned_flat, slot_index.reshape(-1), axis=0).reshape(
        token_count, top_count, returned.shape[2]
    )
    moe_out = jnp.sum(gates[:, :, None] * picked.astype(jnp.float32), axis=1).astype(jnp.bfloat16)
    return (moe_out, attn_latent)


def solution(mesh):
    return jax.shard_map(
        local,
        mesh=mesh,
        in_specs=(
            P(("groups", "ep"), "tp"),
            P(("groups", "ep"), None),
            P("tp", None),
            P("ep", None, "tp"),
            P("ep", None, "tp"),
            P("ep", "tp", None),
            P(("groups", "ep"), "tp", None),
            P(("groups", "ep"), "tp", None),
            P(("groups", "ep"), None, None),
            P(("groups", "ep"), None, None),
            P(("groups", "ep")),
        ),
        out_specs=(P(("groups", "ep"), "tp"), P(("groups", "ep"), "tp", None)),
        check_vma=False,
    )
```

profile of v0, /device:TPU:514, one launch (start us, length us, event | category | flops | bytes accessed | tf_op | source)
XLA Modules:
  0.0 199.2 jit_solution(17828745028653575509)
XLA Ops:
  7.3 0.8 copy.21
  8.3 0.2 reduce_window_sum.11
  8.5 0.2 select_reduce_fusion.2
  8.7 0.1 convert_reduce_fusion
  8.9 1.5 fusion.7
  10.4 66.5 %all_to_all.15 = bf16[64,8,1792]{2,1,0:T(8,128)(2,1)} all-to-all(bf16[64,8,1792]{2,1,0:T(8,128)(2,1)S(1)} %fusion.7), channel_id=1, replica_groups=mesh['groups'=2,'ep'=64,'tp'=2] {'ep'}, dimensions={0} | all-to-all | bytes 3670016 | tf_op jit(solution)/shard_map/all_to_all | solution.py:61
  77.0 6.0 %copy.25 = bf16[3584,512]{1,0:T(8,128)(2,1)} copy(bf16[3584,512]{0,1:T(8,128)(2,1)} %bitcast.59) | data formatting | bytes 7340032 | tf_op jit(solution)/shard_map/dot_general | solution.py:68
  82.9 20.7 %all-gather.3.cloned.1.call-done = bf16[64,8,3584]{2,1,0:T(8,128)(2,1)} async-done(((bf16[64,8,1792]{2,1,0:T(8,128)(2,1)}), bf16[64,8,3584]{2,1,0:T(8,128)(2,1)}) %all-gather.3.cloned.1.call-update) | async-done | bytes 3670032 | tf_op jit(solution)/shard_map/all_gather | solution.py:62
  103.6 5.3 %fusion.3 = f32[512,512]{1,0:T(8,128)S(1)} fusion(bf16[1,3584,512]{2,1,0:T(8,128)(2,1)} %param.14, bf16[64,8,3584]{2,1,0:T(8,128)(2,1)} %all-gather.3.cloned.1.call-done), kind=kOutput, calls=%fused_computation.5 | convolution fusion | flops 1879048192 | bytes 8388608 | tf_op jit(solution)/shard_map/dot_general | solution.py:65
  109.0 2.1 %fusion.18 = bf16[512,512,1]{1,0,2:T(8,128)(2,1)S(1)} fusion(bf16[1,3584,512]{2,1,0:T(8,128)(2,1)S(1)} %copy-done.7, bf16[64,8,3584]{2,1,0:T(8,128)(2,1)S(1)} %copy-done.8, f32[512,512]{1,0:T(8,128)S(1)} %fusion.3), kind=kOutput, calls=%fused_computation.14 | convolution fusion | flops 1880621056 | bytes 8912896 | tf_op jit(solution)/shard_map/dot_general | solution.py:66
  111.2 2.1 %convolution_bitcast_fusion = f32[2,512,1792]{2,1,0:T(8,128)S(1)} fusion(bf16[512,512,1]{1,0,2:T(8,128)(2,1)S(1)} %fusion.18, bf16[2,1792,512]{2,1,0:T(8,128)(2,1)S(1)} %bitcast.57), kind=kOutput, calls=%fused_computation.2 | convolution fusion | flops 1879048192 | bytes 11534336 | tf_op jit(solution)/shard_map/dot_general | solution.py:68
  113.3 10.9 %all_to_all.16 = f32[2,512,1792]{2,1,0:T(8,128)} all-to-all(f32[2,512,1792]{2,1,0:T(8,128)S(1)} %convolution_bitcast_fusion), channel_id=1, replica_groups=mesh['groups'=2,'ep'=64,'tp'=2] {'tp'}, dimensions={0} | all-to-all | bytes 14680064 | tf_op jit(solution)/shard_map/all_to_all | solution.py:23
  124.2 5.5 %reduce_sum.77 = bf16[512,1792]{1,0:T(8,128)(2,1)} reduce(f32[2,512,1792]{2,1,0:T(8,128)} %all_to_all.16, f32[]{:T(128)} %constant.13.clone.1), dimensions={0}, to_apply=%region_6.7 | reduce | flops 917504 | bytes 9175044 | tf_op jit(solution)/shard_map/reduce_sum | solution.py:24
  129.7 13.8 %all-to-all-start.2 = ((bf16[64,8,1792]{2,1,0:T(8,128)(2,1)}), bf16[64,8,1792]{2,1,0:T(8,128)(2,1)S(1)}, u32[]{:S(2)}, u32[]{:S(2)}) async-start(bf16[64,8,1792]{2,1,0:T(8,128)(2,1)} %bitcast.58), calls=%async_computation.2 | async-start | bytes 3670016 | tf_op jit(solution)/shard_map/all_to_all | solution.py:71
  143.6 0.1 fusion.35
  143.8 1.9 all-gather
  145.7 0.3 select_reduce_fusion
  146.1 0.4 fusion.36
  146.5 0.1 fusion.27
  146.7 0.2 fusion.34
  146.9 1.0 convolution_convert_fusion.1
  147.9 42.2 %all-to-all-done.2 = bf16[64,8,1792]{2,1,0:T(8,128)(2,1)S(1)} async-done(((bf16[64,8,1792]{2,1,0:T(8,128)(2,1)}), bf16[64,8,1792]{2,1,0:T(8,128)(2,1)S(1)}, u32[]{:S(2)}, u32[]{:S(2)}) %all-to-all-start.2) | async-done | bytes 1835040 | tf_op jit(solution)/shard_map/all_to_all | solution.py:71
  190.1 0.9 gather_fusion
  191.0 1.3 multiply_reduce_fusion
  (33 shorter events, 0.7 us)
Async XLA Ops:
  7.2 138.9 %copy-start = (bf16[4,256,512]{2,1,0:T(8,128)(2,1)S(1)}, bf16[4,256,512]{2,1,0:T(8,128)(2,1)}, u32[]{:S(2)}) copy-start(bf16[4,256,512]{2,1,0:T(8,128)(2,1)} %param.19) | copy-start | bytes 3145732
  7.2 96.4 %all-gather.3.cloned.1.call-start = ((), (), s32[]{:S(2)}) async-start(), calls=%async_computation.3 | async-start | bytes 5505024 | tf_op jit(solution)/shard_map/all_gather | solution.py:62
  103.6 5.4 %copy-start.7 = (bf16[1,3584,512]{2,1,0:T(8,128)(2,1)S(1)}, bf16[1,3584,512]{2,1,0:T(8,128)(2,1)}, u32[]{:S(2)}) copy-start(bf16[1,3584,512]{2,1,0:T(8,128)(2,1)} %param.15) | copy-start | bytes 11010052
  103.6 5.4 %copy-start.8 = (bf16[64,8,3584]{2,1,0:T(8,128)(2,1)S(1)}, bf16[64,8,3584]{2,1,0:T(8,128)(2,1)}, u32[]{:S(2)}) copy-start(bf16[64,8,3584]{2,1,0:T(8,128)(2,1)} %all-gather.3.cloned.1.call-done) | copy-start | bytes 11010052
  109.0 2.2 %copy-start.1 = (bf16[3584,512]{1,0:T(8,128)(2,1)S(1)}, bf16[3584,512]{1,0:T(8,128)(2,1)}, u32[]{:S(2)}) copy-start(bf16[3584,512]{1,0:T(8,128)(2,1)} %copy.25) | copy-start | bytes 11010052
  129.6 14.0 %copy-start.2 = (bf16[1792,64]{0,1:T(8,128)(2,1)S(1)}, bf16[1792,64]{0,1:T(8,128)(2,1)}, u32[]{:S(2)}) copy-start(bf16[1792,64]{0,1:T(8,128)(2,1)} %param.13) | copy-start | bytes 688132
  129.6 14.0 %copy-start.3 = (bf16[16,1792]{1,0:T(8,128)(2,1)S(1)}, bf16[16,1792]{1,0:T(8,128)(2,1)}, u32[]{:S(2)}) copy-start(bf16[16,1792]{1,0:T(8,128)(2,1)} %param.11) | copy-start | bytes 172036
  129.6 16.4 %copy-start.9 = (s32[4]{0:T(128)S(1)}, s32[4]{0:T(128)}, u32[]{:S(2)}) copy-start(s32[4]{0:T(128)} %param.21) | copy-start | bytes 52
  129.6 16.4 %copy-start.4 = (bf16[4,32,512]{2,1,0:T(8,128)(2,1)S(1)}, bf16[4,32,512]{2,1,0:T(8,128)(2,1)}, u32[]{:S(2)}) copy-start(bf16[4,32,512]{2,1,0:T(8,128)(2,1)} %param.17) | copy-start | bytes 393220
  129.6 16.8 %copy-start.5 = (bf16[4,64,256]{2,1,0:T(8,128)(2,1)S(1)}, bf16[4,64,256]{2,1,0:T(8,128)(2,1)}, u32[]{:S(2)}) copy-start(bf16[4,64,256]{2,1,0:T(8,128)(2,1)} %param.20) | copy-start | bytes 393220
  129.6 16.9 %copy-start.6 = (bf16[4,32,64]{2,1,0:T(8,128)(2,1)S(1)}, bf16[4,32,64]{2,1,0:T(8,128)(2,1)}, u32[]{:S(2)}) copy-start(bf16[4,32,64]{2,1,0:T(8,128)(2,1)} %param.18) | copy-start | bytes 49156
  129.7 60.4 %all-to-all-start.2 = ((bf16[64,8,1792]{2,1,0:T(8,128)(2,1)}), bf16[64,8,1792]{2,1,0:T(8,128)(2,1)S(1)}, u32[]{:S(2)}, u32[]{:S(2)}) async-start(bf16[64,8,1792]{2,1,0:T(8,128)(2,1)} %bitcast.58), calls=%async_computation.2 | async-start | bytes 3670016 | tf_op jit(solution)/shard_map/all_to_all | solution.py:71
Sparse Core Ops, SparseCore 0:
  77.1 26.4 all-gather.2
where the time goes:
time: 200 us; the launch traced here: 199 us
  blocking collectives  79.3 us (40%)
  waiting for transfers between devices  62.9 us (31%)
  between operations  14.2 us (7%)
  starting transfers between devices  13.9 us (7%)
  matrix products  12.8 us (6%)
  local copies, waits for them, and re-layouts  8.03 us (4%)
  other arithmetic  8.02 us (4%)
    all_to_all x1, blocking collectives, local(): lax.all_to_all(outgoing, 'ep', split_axis=0, concat_axis=0, tiled=True)  66.5 us
    all_to_all x1, waiting for transfers between devices, local(): lax.all_to_all(summed, 'ep', split_axis=0, concat_axis=0, tiled=True)  42.2 us
    all_gather x1, waiting for transfers between devices, local(): received = lax.all_gather(received, 'tp', axis=2, tiled=True)  20.7 us
    all_to_all x1, starting transfers between devices, local(): lax.all_to_all(summed, 'ep', split_axis=0, concat_axis=0, tiled=True)  13.8 us
    all_to_all x1, blocking collectives, sum_at_owner(): lax.all_to_all(in_blocks(value, dim, devices), axis, 0, 0, tiled=True)  10.9 us
    dot_general x1, local copies, waits for them, and re-layouts, local(): jnp.dot(active, down_weight[0], preferred_element_type=jnp.float32)  5.96 us
    reduce_sum x1, other arithmetic, sum_at_owner(): return jnp.sum(tiles, axis=0)  5.46 us
    dot_general x1, matrix products, local(): jnp.dot(flat_rows, gate_weight[0], preferred_element_type=jnp.float32)  5.34 us
  transfers between devices with their start and end apart: 2, of which 2 were waited for; matrix products, arithmetic and copies ran while one was open for 4% of the time, Pallas kernels for 0%

commit v1 on v0

--- a/solution.py
+++ b/solution.py
@@ -59,7 +59,11 @@
     outgoing = jnp.dot(placing, hidden, preferred_element_type=jnp.float32).astype(jnp.bfloat16)
     outgoing = outgoing.reshape(expert_count, capacity, hidden.shape[1])
     received = lax.all_to_all(outgoing, "ep", split_axis=0, concat_axis=0, tiled=True)
-    received = lax.all_gather(received, "tp", axis=2, tiled=True)
+    size = lax.axis_size("tp")
+    repeats = [size if d == 2 else 1 for d in range(received.ndim)]
+    received = lax.all_to_all(
+        jnp.tile(received, repeats), "tp", split_axis=2, concat_axis=2, tiled=True
+    )
     source_count, slot_count, feature_count = received.shape
     flat_rows = received.reshape(source_count * slot_count, feature_count)
     gate_part = jnp.dot(flat_rows, gate_weight[0], preferred_element_type=jnp.float32)

time: 200 us -> 208 us (1.040)
  blocking collectives: 79.3 us -> 24 us
  local copies, waits for them, and re-layouts: 8.03 us -> 47.1 us
  starting transfers between devices: 13.9 us -> 33.7 us
  waiting for transfers between devices: 62.9 us -> 78.6 us
  between operations: 14.2 us -> 0.83 us
    all_to_all x1, blocking collectives: 66.5 us -> 11.3 us  [local(): lax.all_to_all(jnp.tile(received, repeats), 'tp', split_axis=2, concat_ax...]
    all_to_all x0 -> x1, waiting for transfers between devices: none -> 36.4 us  [local(): lax.all_to_all(outgoing, 'ep', split_axis=0, concat_axis=0, tiled=True)]
    all_to_all x0 -> x1, starting transfers between devices: none -> 24.3 us  [local(): lax.all_to_all(outgoing, 'ep', split_axis=0, concat_axis=0, tiled=True)]
    all_gather x1 -> x0, waiting for transfers between devices: 20.7 us -> none  [local(): received = lax.all_gather(received, 'tp', axis=2, tiled=True)]
    unnamed x21 -> x23, local copies, waits for them, and re-layouts: 0.89 us -> 18.7 us
    all_to_all x0 -> x2, local copies, waits for them, and re-layouts: none -> 15.8 us  [the longest x1 10.8 us: local(): lax.all_to_all(jnp.tile(received, repeats), 'tp', split_axis=2, concat_ax...]
    another operation x0 -> x1, local copies, waits for them, and re-layouts: none -> 5.5 us  [local(): jnp.tile(received, repeats)]
    all_to_all x1, starting transfers between devices: 13.8 us -> 9.46 us  [local(): lax.all_to_all(summed, 'ep', split_axis=0, concat_axis=0, tiled=True)]
where the time goes in v1:
time: 208 us; the launch traced here: 206 us
  waiting for transfers between devices  78.6 us (38%)
  local copies, waits for them, and re-layouts  47.1 us (23%)
  starting transfers between devices  33.7 us (16%)
  blocking collectives  24 us (12%)
  matrix products  14 us (7%)
  other arithmetic  8.02 us (4%)
    all_to_all x1, waiting for transfers between devices, local(): lax.all_to_all(summed, 'ep', split_axis=0, concat_axis=0, tiled=True)  42.2 us
    all_to_all x1, waiting for transfers between devices, local(): lax.all_to_all(outgoing, 'ep', split_axis=0, concat_axis=0, tiled=True)  36.4 us
    all_to_all x1, starting transfers between devices, local(): lax.all_to_all(outgoing, 'ep', split_axis=0, concat_axis=0, tiled=True)  24.3 us
    unnamed x23, local copies, waits for them, and re-layouts  18.7 us
    all_to_all x1, blocking collectives, local(): lax.all_to_all(jnp.tile(received, repeats), 'tp', split_axis=2, concat_ax...  11.3 us
    all_to_all x1, blocking collectives, sum_at_owner(): lax.all_to_all(in_blocks(value, dim, devices), axis, 0, 0, tiled=True)  10.9 us
    all_to_all x1, local copies, waits for them, and re-layouts, local(): lax.all_to_all(jnp.tile(received, repeats), 'tp', split_axis=2, concat_ax...  10.8 us
    all_to_all x1, starting transfers between devices, local(): lax.all_to_all(summed, 'ep', split_axis=0, concat_axis=0, tiled=True)  9.46 us
  transfers between devices with their start and end apart: 2, of which 2 were waited for; matrix products, arithmetic and copies ran while one was open for 4% of the time, Pallas kernels for 0%

profile of v1, /device:TPU:514, one launch (start us, length us, event | category | flops | bytes accessed | tf_op | source)
XLA Modules:
  0.0 206.3 jit_solution(7679050676466049725)
XLA Ops:
  0.6 0.8 copy.38
  2.3 2.7 %fusion.7 = bf16[64,8,1792]{2,1,0:T(8,128)(2,1)} fusion(bf16[16,1792]{1,0:T(8,128)(2,1)} %param.11, s32[512,16]{0,1:T(8,128)S(1)} %convert_reduce_fusion), kind=kOutput, calls=%fused_computation.10 | convolution fusion | flops 30285824 | bytes 1925120 | tf_op jit(solution)/shard_map/dot_general | solution.py:59
  5.0 24.3 %all-to-all-start = ((bf16[64,8,1792]{2,1,0:T(8,128)(2,1)}), bf16[64,8,1792]{2,1,0:T(8,128)(2,1)S(1)}, u32[]{:S(2)}, u32[]{:S(2)}) async-start(bf16[64,8,1792]{2,1,0:T(8,128)(2,1)} %fusion.7), calls=%async_computation | async-start | bytes 3670016 | tf_op jit(solution)/shard_map/all_to_all | solution.py:61
  29.3 6.0 %copy.44 = bf16[3584,512]{1,0:T(8,128)(2,1)} copy(bf16[3584,512]{0,1:T(8,128)(2,1)} %bitcast.64) | data formatting | bytes 7340032 | tf_op jit(solution)/shard_map/dot_general | solution.py:72
  35.3 36.4 %all-to-all-done = bf16[64,8,1792]{2,1,0:T(8,128)(2,1)S(1)} async-done(((bf16[64,8,1792]{2,1,0:T(8,128)(2,1)}), bf16[64,8,1792]{2,1,0:T(8,128)(2,1)S(1)}, u32[]{:S(2)}, u32[]{:S(2)}) %all-to-all-start) | async-done | bytes 1835040 | tf_op jit(solution)/shard_map/all_to_all | solution.py:61
  71.7 5.0 %copy.41 = bf16[64,8,1792]{0,1,2:T(8,128)(2,1)} copy(bf16[64,8,1792]{2,1,0:T(8,128)(2,1)S(1)} %all-to-all-done) | data formatting | bytes 3670016 | tf_op jit(solution)/shard_map/all_to_all | solution.py:61
  76.7 5.5 %tile.4 = bf16[64,8,2,1792]{0,1,3,2:T(8,128)(2,1)} broadcast(bf16[64,8,1792]{0,1,2:T(8,128)(2,1)} %copy.41), dimensions={0,1,3} | broadcast | bytes 5505024 | tf_op jit(solution)/shard_map/tile | solution.py:65
  82.2 9.0 %reshape.135 = bf16[2,2,458752]{2,1,0:T(2,128)(2,1)} reshape(bf16[3584,8,64]{2,1,0:T(8,128)(2,1)} %bitcast.59) | data formatting | bytes 7340032
  91.2 11.3 %all_to_all.20 = bf16[2,2,458752]{2,1,0:T(2,128)(2,1)} all-to-all(bf16[2,2,458752]{2,1,0:T(2,128)(2,1)} %reshape.135), channel_id=1, replica_groups=mesh['groups'=2,'ep'=64,'tp'=2] {'tp'}, dimensions={0} | all-to-all | bytes 7340032 | tf_op jit(solution)/shard_map/all_to_all | solution.py:64
  102.5 8.8 %reshape.136 = bf16[3584,8,64]{2,1,0:T(8,128)(2,1)} reshape(bf16[2,2,458752]{2,1,0:T(2,128)(2,1)} %all_to_all.20) | data formatting | bytes 7340032
  111.2 10.8 %copy.42 = bf16[64,8,3584]{2,1,0:T(8,128)(2,1)} copy(bf16[64,8,3584]{0,1,2:T(8,128)(2,1)} %bitcast.60) | data formatting | bytes 7340032 | tf_op jit(solution)/shard_map/all_to_all | solution.py:64
  122.0 5.3 %fusion.3 = f32[512,512]{1,0:T(8,128)S(1)} fusion(bf16[1,3584,512]{2,1,0:T(8,128)(2,1)} %param.14, bf16[64,8,3584]{2,1,0:T(8,128)(2,1)} %copy.42), kind=kOutput, calls=%fused_computation.5 | convolution fusion | flops 1879048192 | bytes 8388608 | tf_op jit(solution)/shard_map/dot_general | solution.py:69
  127.4 2.1 %fusion.18 = bf16[512,512,1]{1,0,2:T(8,128)(2,1)S(1)} fusion(bf16[1,3584,512]{2,1,0:T(8,128)(2,1)S(1)} %copy-done.8, bf16[64,8,3584]{2,1,0:T(8,128)(2,1)S(1)} %copy-done.2, f32[512,512]{1,0:T(8,128)S(1)} %fusion.3), kind=kOutput, calls=%fused_computation.14 | convolution fusion | flops 1880621056 | bytes 8912896 | tf_op jit(solution)/shard_map/dot_general | solution.py:70
  129.6 2.1 %convolution_bitcast_fusion = f32[2,512,1792]{2,1,0:T(8,128)S(1)} fusion(bf16[512,512,1]{1,0,2:T(8,128)(2,1)S(1)} %fusion.18, bf16[2,1792,512]{2,1,0:T(8,128)(2,1)S(1)} %bitcast.62), kind=kOutput, calls=%fused_computation.2 | convolution fusion | flops 1879048192 | bytes 11534336 | tf_op jit(solution)/shard_map/dot_general | solution.py:72
  131.7 10.9 %all_to_all.21 = f32[2,512,1792]{2,1,0:T(8,128)} all-to-all(f32[2,512,1792]{2,1,0:T(8,128)S(1)} %convolution_bitcast_fusion), channel_id=1, replica_groups=mesh['groups'=2,'ep'=64,'tp'=2] {'tp'}, dimensions={0} | all-to-all | bytes 14680064 | tf_op jit(solution)/shard_map/all_to_all | solution.py:23
  142.6 5.5 %reduce_sum.77 = bf16[512,1792]{1,0:T(8,128)(2,1)} reduce(f32[2,512,1792]{2,1,0:T(8,128)} %all_to_all.21, f32[]{:T(128)} %constant.13.clone.1), dimensions={0}, to_apply=%region_6.7 | reduce | flops 917504 | bytes 9175044 | tf_op jit(solution)/shard_map/reduce_sum | solution.py:24
  148.1 9.5 %all-to-all-start.3 = ((bf16[64,8,1792]{2,1,0:T(8,128)(2,1)}), bf16[64,8,1792]{2,1,0:T(8,128)(2,1)S(1)}, u32[]{:S(2)}, u32[]{:S(2)}) async-start(bf16[64,8,1792]{2,1,0:T(8,128)(2,1)} %bitcast.63), calls=%async_computation.3 | async-start | bytes 3670016 | tf_op jit(solution)/shard_map/all_to_all | solution.py:75
  157.8 1.9 all-gather
  159.7 0.3 select_reduce_fusion
  160.1 0.4 fusion.36
  160.9 1.0 convolution_convert_fusion.1
  161.9 42.2 %all-to-all-done.3 = bf16[64,8,1792]{2,1,0:T(8,128)(2,1)S(1)} async-done(((bf16[64,8,1792]{2,1,0:T(8,128)(2,1)}), bf16[64,8,1792]{2,1,0:T(8,128)(2,1)S(1)}, u32[]{:S(2)}, u32[]{:S(2)}) %all-to-all-start.3) | async-done | bytes 1835040 | tf_op jit(solution)/shard_map/all_to_all | solution.py:75
  204.1 0.9 gather_fusion
  205.0 1.3 multiply_reduce_fusion
  (37 shorter events, 1.6 us)
Async XLA Ops:
  0.6 159.5 %copy-start = (bf16[4,256,512]{2,1,0:T(8,128)(2,1)S(1)}, bf16[4,256,512]{2,1,0:T(8,128)(2,1)}, u32[]{:S(2)}) copy-start(bf16[4,256,512]{2,1,0:T(8,128)(2,1)} %param.19) | copy-start | bytes 3145732
  5.0 66.7 %all-to-all-start = ((bf16[64,8,1792]{2,1,0:T(8,128)(2,1)}), bf16[64,8,1792]{2,1,0:T(8,128)(2,1)S(1)}, u32[]{:S(2)}, u32[]{:S(2)}) async-start(bf16[64,8,1792]{2,1,0:T(8,128)(2,1)} %fusion.7), calls=%async_computation | async-start | bytes 3670016 | tf_op jit(solution)/shard_map/all_to_all | solution.py:61
  122.0 5.4 %copy-start.2 = (bf16[64,8,3584]{2,1,0:T(8,128)(2,1)S(1)}, bf16[64,8,3584]{2,1,0:T(8,128)(2,1)}, u32[]{:S(2)}) copy-start(bf16[64,8,3584]{2,1,0:T(8,128)(2,1)} %copy.42) | copy-start | bytes 11010052
  122.0 5.4 %copy-start.8 = (bf16[1,3584,512]{2,1,0:T(8,128)(2,1)S(1)}, bf16[1,3584,512]{2,1,0:T(8,128)(2,1)}, u32[]{:S(2)}) copy-start(bf16[1,3584,512]{2,1,0:T(8,128)(2,1)} %param.15) | copy-start | bytes 11010052
  127.4 2.2 %copy-start.1 = (bf16[3584,512]{1,0:T(8,128)(2,1)S(1)}, bf16[3584,512]{1,0:T(8,128)(2,1)}, u32[]{:S(2)}) copy-start(bf16[3584,512]{1,0:T(8,128)(2,1)} %copy.44) | copy-start | bytes 11010052
  148.0 9.6 %copy-start.3 = (bf16[1792,64]{0,1:T(8,128)(2,1)S(1)}, bf16[1792,64]{0,1:T(8,128)(2,1)}, u32[]{:S(2)}) copy-start(bf16[1792,64]{0,1:T(8,128)(2,1)} %param.13) | copy-start | bytes 688132
  148.0 9.6 %copy-start.4 = (bf16[16,1792]{1,0:T(8,128)(2,1)S(1)}, bf16[16,1792]{1,0:T(8,128)(2,1)}, u32[]{:S(2)}) copy-start(bf16[16,1792]{1,0:T(8,128)(2,1)} %param.11) | copy-start | bytes 172036
  148.0 12.0 %copy-start.9 = (s32[4]{0:T(128)S(1)}, s32[4]{0:T(128)}, u32[]{:S(2)}) copy-start(s32[4]{0:T(128)} %param.21) | copy-start | bytes 52
  148.0 12.1 %copy-start.5 = (bf16[4,32,512]{2,1,0:T(8,128)(2,1)S(1)}, bf16[4,32,512]{2,1,0:T(8,128)(2,1)}, u32[]{:S(2)}) copy-start(bf16[4,32,512]{2,1,0:T(8,128)(2,1)} %param.17) | copy-start | bytes 393220
  148.0 12.5 %copy-start.6 = (bf16[4,64,256]{2,1,0:T(8,128)(2,1)S(1)}, bf16[4,64,256]{2,1,0:T(8,128)(2,1)}, u32[]{:S(2)}) copy-start(bf16[4,64,256]{2,1,0:T(8,128)(2,1)} %param.20) | copy-start | bytes 393220
  148.0 12.5 %copy-start.7 = (bf16[4,32,64]{2,1,0:T(8,128)(2,1)S(1)}, bf16[4,32,64]{2,1,0:T(8,128)(2,1)}, u32[]{:S(2)}) copy-start(bf16[4,32,64]{2,1,0:T(8,128)(2,1)} %param.18) | copy-start | bytes 49156
  148.1 56.1 %all-to-all-start.3 = ((bf16[64,8,1792]{2,1,0:T(8,128)(2,1)}), bf16[64,8,1792]{2,1,0:T(8,128)(2,1)S(1)}, u32[]{:S(2)}, u32[]{:S(2)}) async-start(bf16[64,8,1792]{2,1,0:T(8,128)(2,1)} %bitcast.63), calls=%async_computation.3 | async-start | bytes 3670016 | tf_op jit(solution)/shard_map/all_to_all | solution.py:75
